TPU v7x, 32 devices: a whole 2x2x4 slice. The times are simulated.
32 devices in a mesh: up: 8 (over y, x, core), dn: 4 (over z).
Axes of the slice: x: 2, y: 2, z: 4, core: 2. Of those that a mesh axis runs over, the one named last changes fastest.
Arguments:
- start_vector: bfloat16 [13312, 13312], P('up', 'dn'), may hold values from -6 to 6
- hop_tiles: bfloat16 [104, 5, 128, 128], replicated, may hold values from -0.5 to 0.5
- tile_columns: int32 [104, 5], replicated, may hold values from 0 to 103, as said below
- tile_signs: int32 [104, 5], replicated, may hold values from 0 to 1
- occupation: int32 [16, 13312], replicated, may hold values from 0 to 1, as said below
Outputs:
- next_vector: bfloat16 [13312, 13312], P('up', 'dn')
- alphas: float32 [2], replicated
- betas: float32 [2], replicated
Inputs may be any that keep to these rules, and one draw needn't show every extreme that they name: Each row of tile_columns names 5 different tile columns. Every column of occupation holds exactly 8 ones.
All inputs are finite; a program needn't handle non-finite values.
Results may differ from a plain program's by a relative error of at most 0.0065.
Values may be sent and summed in bfloat16 or wider, within the bound.
A program may use at most 256 MiB of HBM per device.

v0:
```python
import jax
import jax.numpy as jnp
from jax import lax
from jax.sharding import PartitionSpec as P

STEPS = 2
coupling = 4.0


def hop_lead(matrix, signed, tile_columns):
    layout = matrix.shape
    tile_width = signed.shape[-1]
    cube = matrix.reshape(layout[0] // tile_width, tile_width, -1)
    picked = cube[tile_columns]
    result = jnp.einsum("ikab,ikbm->iam", signed, picked, preferred_element_type=jnp.float32)
    return result.reshape(layout).astype(jnp.bfloat16)


def body(start_vector, hop_tiles, tile_columns, tile_signs, occupation):
    signed = hop_tiles * (1 - 2 * tile_signs).astype(jnp.bfloat16)[:, :, None, None]
    rows_local, cols_local = start_vector.shape
    count_up = lax.axis_size("up")
    count_down = lax.axis_size("dn")
    row_start = lax.axis_index("up") * rows_local
    col_start = lax.axis_index("dn") * cols_local
    block_rows, block_cols = start_vector.shape
    occ_rows = lax.dynamic_slice_in_dim(occupation, row_start, block_rows, 1).astype(jnp.bfloat16)
    occ_cols = lax.dynamic_slice_in_dim(occupation, col_start, block_cols, 1).astype(jnp.bfloat16)
    diagonal = coupling * jnp.einsum(
        "sa,sb->ab", occ_rows, occ_cols, preferred_element_type=jnp.float32
    )
    vector = start_vector.astype(jnp.float32)
    total = lax.psum(jnp.sum(vector * vector), ("up", "dn"))
    vector = vector / jnp.maximum(jnp.sqrt(total), 1.0)
    length = total / jnp.maximum(total, 1.0)
    previous = jnp.zeros_like(vector)
    beta_value = jnp.float32(0.0)
    alpha_list = []
    beta_list = []
    for iteration in range(STEPS):
        rounded = vector.astype(jnp.bfloat16)
        cube = rounded.reshape(block_rows, count_up, block_cols // count_up)
        up_part = lax.all_to_all(cube, "up", split_axis=1, concat_axis=0, tiled=True)
        up_whole = up_part.reshape(up_part.shape[0], up_part.shape[2])
        up_hopped = hop_lead(up_whole, signed, tile_columns).reshape(up_part.shape)
        moved = lax.all_to_all(up_hopped, "up", split_axis=0, concat_axis=1, tiled=True)
        hopped_up = moved.reshape(block_rows, block_cols)
        flipped = rounded.T.reshape(block_cols, count_down, block_rows // count_down)
        part = lax.all_to_all(flipped, "dn", split_axis=1, concat_axis=0, tiled=True)
        whole = part.reshape(part.shape[0], part.shape[2])
        hopped = hop_lead(whole, signed, tile_columns).reshape(part.shape)
        returned = lax.all_to_all(hopped, "dn", split_axis=0, concat_axis=1, tiled=True)
        hopped_down = returned.reshape(block_cols, block_rows).T
        work = (
            hopped_up.astype(jnp.float32)
            + hopped_down.astype(jnp.float32)
            + diagonal * vector
            - beta_value * previous
        )
        intersect, square = lax.psum((jnp.sum(work * vector), jnp.sum(work * work)), ("up", "dn"))
        work = work - intersect * vector
        residual = square - 2.0 * intersect * intersect + intersect * intersect * length
        beta_value = jnp.sqrt(jnp.maximum(residual, 1.0))
        length = residual / jnp.maximum(residual, 1.0)
        previous = vector
        vector = work / beta_value
        alpha_list.append(intersect)
        beta_list.append(beta_value)
    final = vector.astype(jnp.bfloat16)
    return (final, jnp.stack(alpha_list), jnp.stack(beta_list))


def solution(mesh):
    placed = (P("up", "dn"), P(), P(), P(), P())
    return jax.shard_map(
        body, mesh=mesh, in_specs=placed, out_specs=(P("up", "dn"), P(), P()), check_vma=False
    )
```

profile of v0, /device:TPU:12, one launch (start us, length us, event | category | flops | bytes accessed | tf_op | source)
XLA Modules:
  0.0 2605.0 jit_solution(15196336587195113989)
XLA Ops:
  11.1 41.6 %psum.35 = f32[]{:T(128)} all-reduce(f32[]{:T(128)} %fusion), channel_id=1, replica_groups=mesh['up'=8,'dn'=4] {'up','dn'}, use_global_device_ids=true, to_apply=%region_1.0 | all-reduce | flops 1 | bytes 8 | tf_op jit(solution)/shard_map/psum | solution.py:33
  80.3 127.1 %all_to_all.96 = bf16[1664,8,416]{0,2,1:T(8,128)(2,1)} all-to-all(bf16[1664,8,416]{0,2,1:T(8,128)(2,1)} %bitcast.112), channel_id=1, replica_groups=mesh['up'=8,'dn'=4] {'up'}, dimensions={1} | all-to-all | bytes 22151168 | tf_op jit(solution)/shard_map/all_to_all | solution.py:43
  337.4 77.7 %reshape.155 = bf16[13312,1,416]{2,1,0:T(2,128)(2,1)} reshape(bf16[104,128,416]{2,1,0:T(8,128)(2,1)} %copy.95) | data formatting | bytes 22151168 | tf_op jit(solution)/shard_map/convert_element_type | solution.py:16
  415.7 87.5 %reduce = bf16[13312,416]{1,0:T(8,128)(2,1)} reduce(bf16[13312,1,416]{2,1,0:T(2,128)(2,1)} %reshape.155, bf16[]{:T(256)} %broadcast.21), dimensions={1}, to_apply=%reshape.155.reduce_sub_computation | reduce | bytes 22151170 | tf_op jit(solution)/shard_map/convert_element_type | solution.py:16
  659.6 77.6 %reshape.156 = bf16[13312,1,416]{2,1,0:T(2,128)(2,1)} reshape(bf16[104,128,416]{2,1,0:T(8,128)(2,1)} %copy.96) | data formatting | bytes 22151168 | tf_op jit(solution)/shard_map/convert_element_type | solution.py:16
  737.1 87.6 %reduce.1 = bf16[13312,416]{1,0:T(8,128)(2,1)} reduce(bf16[13312,1,416]{2,1,0:T(2,128)(2,1)} %reshape.156, bf16[]{:T(256)} %broadcast.21), dimensions={1}, to_apply=%reshape.156.reduce_sub_computation | reduce | bytes 22151170 | tf_op jit(solution)/shard_map/convert_element_type | solution.py:16
  854.8 30.4 %reshape.160 = bf16[13312,1,416]{2,1,0:T(2,128)(2,1)} reshape(bf16[8,2,346112]{2,1,0:T(2,128)(2,1)} %all-to-all-done.1) | data formatting | bytes 22151168
  885.3 52.5 %copy.68 = bf16[13312,1,416]{0,2,1:T(8,128)(2,1)} copy(bf16[13312,1,416]{2,1,0:T(2,128)(2,1)} %reshape.160) | data formatting | bytes 22151168 | tf_op jit(solution)/shard_map/all_to_all | solution.py:46
  995.2 96.4 %all-to-all-done.3 = bf16[4,2,692224]{2,1,0:T(2,128)(2,1)} async-done(((bf16[4,2,692224]{2,1,0:T(2,128)(2,1)}), bf16[4,2,692224]{2,1,0:T(2,128)(2,1)}, u32[]{:S(2)}, u32[]{:S(2)}) %all-to-all-start.3) | async-done | bytes 11075616 | tf_op jit(solution)/shard_map/all_to_all | solution.py:52
  1091.6 45.3 %reshape.162 = bf16[13312,1,416]{2,1,0:T(2,128)(2,1)} reshape(bf16[4,2,692224]{2,1,0:T(2,128)(2,1)} %all-to-all-done.3) | data formatting | bytes 22151168
  1136.9 52.8 %copy.74 = bf16[13312,1,416]{0,2,1:T(8,128)(2,1)} copy(bf16[13312,1,416]{2,1,0:T(2,128)(2,1)} %reshape.162) | data formatting | bytes 22151168 | tf_op jit(solution)/shard_map/all_to_all | solution.py:52
  1230.7 32.3 %multiply_reduce_fusion.3 = (f32[]{:T(128)}, f32[]{:T(128)}, f32[1664,3328]{1,0:T(8,128)}, f32[1664,3328]{1,0:T(8,128)}) fusion(f32[]{:T(128)S(6)} %max.13, bf16[1664,3328]{1,0:T(8,128)(2,1)} %param.5, f32[1664,3328]{1,0:T(8,128)} %copy.76, f32[3328,4,1,416]{0,3,1,2:T(8,128)} %copy.75, s32[16,13312]{1,0:T(8,128)} %param.9, s32[]{:T(128)S(6)} %select_n.14, ...), kind=kOutput, calls=%fused_computation.21 | convolution fusion | flops 232667136 | bytes 99999760 | tf_op jit(solution)/shard_map/sa,sb->ab/dot_general | solution.py:29
  1263.1 43.3 %all-reduce.1 = (f32[]{:T(128)}, f32[]{:T(128)}) all-reduce(f32[]{:T(128)} %get-tuple-element.6, f32[]{:T(128)} %get-tuple-element.5), channel_id=1, replica_groups=mesh['up'=8,'dn'=4] {'up','dn'}, use_global_device_ids=true, to_apply=%region_5.0 | all-reduce | flops 2 | bytes 16 | tf_op jit(solution)/shard_map/psum | solution.py:60
  1348.6 127.0 %all_to_all.97 = bf16[1664,8,416]{0,2,1:T(8,128)(2,1)} all-to-all(bf16[1664,8,416]{0,2,1:T(8,128)(2,1)} %bitcast.113), channel_id=1, replica_groups=mesh['up'=8,'dn'=4] {'up'}, dimensions={1} | all-to-all | bytes 22151168 | tf_op jit(solution)/shard_map/all_to_all | solution.py:43
  1604.5 77.7 %reshape.157 = bf16[13312,1,416]{2,1,0:T(2,128)(2,1)} reshape(bf16[104,128,416]{2,1,0:T(8,128)(2,1)} %copy.97) | data formatting | bytes 22151168 | tf_op jit(solution)/shard_map/convert_element_type | solution.py:16
  1682.3 87.5 %reduce.2 = bf16[13312,416]{1,0:T(8,128)(2,1)} reduce(bf16[13312,1,416]{2,1,0:T(2,128)(2,1)} %reshape.157, bf16[]{:T(256)} %broadcast.21), dimensions={1}, to_apply=%reshape.157.reduce_sub_computation | reduce | bytes 22151170 | tf_op jit(solution)/shard_map/convert_element_type | solution.py:16
  1926.1 77.6 %reshape.158 = bf16[13312,1,416]{2,1,0:T(2,128)(2,1)} reshape(bf16[104,128,416]{2,1,0:T(8,128)(2,1)} %copy.98) | data formatting | bytes 22151168 | tf_op jit(solution)/shard_map/convert_element_type | solution.py:16
  2003.7 87.6 %reduce.3 = bf16[13312,416]{1,0:T(8,128)(2,1)} reduce(bf16[13312,1,416]{2,1,0:T(2,128)(2,1)} %reshape.158, bf16[]{:T(256)} %broadcast.21), dimensions={1}, to_apply=%reshape.158.reduce_sub_computation | reduce | bytes 22151170 | tf_op jit(solution)/shard_map/convert_element_type | solution.py:16
  2150.5 52.5 %copy.82 = bf16[13312,1,416]{0,2,1:T(8,128)(2,1)} copy(bf16[13312,1,416]{2,1,0:T(2,128)(2,1)} %reshape.164) | data formatting | bytes 22151168 | tf_op jit(solution)/shard_map/all_to_all | solution.py:46
  2260.5 97.7 %all-to-all-done.7 = bf16[4,2,692224]{2,1,0:T(2,128)(2,1)} async-done(((bf16[4,2,692224]{2,1,0:T(2,128)(2,1)}), bf16[4,2,692224]{2,1,0:T(2,128)(2,1)}, u32[]{:S(2)}, u32[]{:S(2)}) %all-to-all-start.7) | async-done | bytes 11075616 | tf_op jit(solution)/shard_map/all_to_all | solution.py:52
  2358.2 45.3 %reshape.166 = bf16[13312,1,416]{2,1,0:T(2,128)(2,1)} reshape(bf16[4,2,692224]{2,1,0:T(2,128)(2,1)} %all-to-all-done.7) | data formatting | bytes 22151168
  2403.5 52.7 %copy.88 = bf16[13312,1,416]{0,2,1:T(8,128)(2,1)} copy(bf16[13312,1,416]{2,1,0:T(2,128)(2,1)} %reshape.166) | data formatting | bytes 22151168 | tf_op jit(solution)/shard_map/all_to_all | solution.py:52
  2497.1 40.2 %multiply_reduce_fusion.1 = (f32[]{:T(128)}, f32[]{:T(128)}, f32[1664,3328]{1,0:T(8,128)}) fusion(f32[1664,3328]{1,0:T(8,128)} %get-tuple-element.13, f32[]{:T(128)S(6)} %max.13, bf16[1664,3328]{1,0:T(8,128)(2,1)} %param.5, f32[]{:T(128)} %sqrt.10, f32[1664,3328]{1,0:T(8,128)} %get-tuple-element.15, f32[1664,3328]{1,0:T(8,128)} %copy.90, ...), kind=kLoop, calls=%fused_computation.18 | loop fusion | flops 66453504 | bytes 121831440 | tf_op jit(solution)/shard_map/reduce_sum | solution.py:60
  2537.3 42.5 %all-reduce = (f32[]{:T(128)}, f32[]{:T(128)}) all-reduce(f32[]{:T(128)} %get-tuple-element.4, f32[]{:T(128)} %get-tuple-element.3), channel_id=1, replica_groups=mesh['up'=8,'dn'=4] {'up','dn'}, use_global_device_ids=true, to_apply=%region_9.0 | all-reduce | flops 2 | bytes 16 | tf_op jit(solution)/shard_map/psum | solution.py:60
  (77 shorter events, 954.8 us)
Async XLA Ops:
  80.3 133.9 %copy-start.4 = (s32[104,5]{0,1:T(8,128)S(1)}, s32[104,5]{0,1:T(8,128)}, u32[]{:S(2)}) copy-start(s32[104,5]{0,1:T(8,128)} %param.8) | copy-start | bytes 6244
  80.3 134.0 %copy-start.5 = (s32[104,5]{0,1:T(8,128)S(1)}, s32[104,5]{0,1:T(8,128)}, u32[]{:S(2)}) copy-start(s32[104,5]{0,1:T(8,128)} %param.7) | copy-start | bytes 6244
  207.5 317.4 %all-to-all-start.2 = ((bf16[3328,4,416]{0,2,1:T(8,128)(2,1)}), bf16[3328,4,416]{0,2,1:T(8,128)(2,1)}, u32[]{:S(2)}, u32[]{:S(2)}) async-start(bf16[3328,4,416]{0,2,1:T(8,128)(2,1)} %bitcast.96), calls=%async_computation.2 | async-start | bytes 22151168 | tf_op jit(solution)/shard_map/all_to_all | solution.py:49
  214.3 399.5 %copy-start.2 = (bf16[104,5]{1,0:T(8,128)(2,1)}, bf16[104,5]{1,0:T(8,128)(2,1)S(1)}, u32[]{:S(2)}) copy-start(bf16[104,5]{1,0:T(8,128)(2,1)S(1)} %copy.61) | copy-start | bytes 3124
  214.7 372.7 %copy-start = (s32[1024]{0:T(1024)}, s32[1024]{0:T(1024)S(1)}, u32[]{:S(2)}) copy-start(s32[1024]{0:T(1024)S(1)} %pad_clamp_fusion) | copy-start | bytes 12292
  524.9 322.3 %all-to-all-start.1 = ((bf16[8,2,346112]{2,1,0:T(2,128)(2,1)}), bf16[8,2,346112]{2,1,0:T(2,128)(2,1)}, u32[]{:S(2)}, u32[]{:S(2)}) async-start(bf16[8,2,346112]{2,1,0:T(2,128)(2,1)} %reshape.159), calls=%async_computation.1 | async-start | bytes 22151168 | tf_op jit(solution)/shard_map/all_to_all | solution.py:46
  847.2 244.5 %all-to-all-start.3 = ((bf16[4,2,692224]{2,1,0:T(2,128)(2,1)}), bf16[4,2,692224]{2,1,0:T(2,128)(2,1)}, u32[]{:S(2)}, u32[]{:S(2)}) async-start(bf16[4,2,692224]{2,1,0:T(2,128)(2,1)} %reshape.161), calls=%async_computation.3 | async-start | bytes 22151168 | tf_op jit(solution)/shard_map/all_to_all | solution.py:52
  1475.6 315.9 %all-to-all-start.6 = ((bf16[3328,4,416]{0,2,1:T(8,128)(2,1)}), bf16[3328,4,416]{0,2,1:T(8,128)(2,1)}, u32[]{:S(2)}, u32[]{:S(2)}) async-start(bf16[3328,4,416]{0,2,1:T(8,128)(2,1)} %bitcast.97), calls=%async_computation.6 | async-start | bytes 22151168 | tf_op jit(solution)/shard_map/all_to_all | solution.py:49
  1500.6 31.8 %copy-start.1 = (s32[1024]{0:T(1024)S(1)}, s32[1024]{0:T(1024)}, u32[]{:S(2)}) copy-start(s32[1024]{0:T(1024)} %copy-done) | copy-start | bytes 12292
  1532.3 26.5 %copy-start.3 = (bf16[104,5]{1,0:T(8,128)(2,1)S(1)}, bf16[104,5]{1,0:T(8,128)(2,1)}, u32[]{:S(2)}) copy-start(bf16[104,5]{1,0:T(8,128)(2,1)} %copy-done.2) | copy-start | bytes 3124
  1791.5 322.3 %all-to-all-start.5 = ((bf16[8,2,346112]{2,1,0:T(2,128)(2,1)}), bf16[8,2,346112]{2,1,0:T(2,128)(2,1)}, u32[]{:S(2)}, u32[]{:S(2)}) async-start(bf16[8,2,346112]{2,1,0:T(2,128)(2,1)} %reshape.163), calls=%async_computation.5 | async-start | bytes 22151168 | tf_op jit(solution)/shard_map/all_to_all | solution.py:46
  2113.7 244.5 %all-to-all-start.7 = ((bf16[4,2,692224]{2,1,0:T(2,128)(2,1)}), bf16[4,2,692224]{2,1,0:T(2,128)(2,1)}, u32[]{:S(2)}, u32[]{:S(2)}) async-start(bf16[4,2,692224]{2,1,0:T(2,128)(2,1)} %reshape.165), calls=%async_computation.7 | async-start | bytes 22151168 | tf_op jit(solution)/shard_map/all_to_all | solution.py:52
where the time goes:
time: 2630 us; the launch traced here: 2600 us
  local copies, waits for them, and re-layouts  1360 us (52%)
  other arithmetic  469 us (18%)
  blocking collectives  381 us (14%)
  waiting for transfers between devices  194 us (7%)
  matrix products  150 us (6%)
  starting transfers between devices  39.6 us (2%)
    convert_element_type x9, local copies, waits for them, and re-layouts, hop_lead(): return result.reshape(layout).astype(jnp.bfloat16)  376 us
    convert_element_type x4, other arithmetic, hop_lead(): return result.reshape(layout).astype(jnp.bfloat16)  350 us
    unnamed x22, local copies, waits for them, and re-layouts  257 us
    all_to_all x2, blocking collectives, body(): lax.all_to_all(cube, 'up', split_axis=1, concat_axis=0, tiled=True)  254 us
    all_to_all x2, waiting for transfers between devices, body(): lax.all_to_all(hopped, 'dn', split_axis=0, concat_axis=1, tiled=True)  194 us
    another operation x8, local copies, waits for them, and re-layouts, hop_lead(): cube = matrix.reshape(layout[0] // tile_width, tile_width, -1)  122 us
    dot_general x4, matrix products, hop_lead(): jnp.einsum('ikab,ikbm->iam', signed, picked, preferred_element_type=jnp.f...  118 us
    gather x4, local copies, waits for them, and re-layouts, hop_lead(): picked = cube[tile_columns]  106 us
  transfers between devices with their start and end apart: 6, of which 2 were waited for; matrix products, arithmetic and copies ran while one was open for 59% of the time, Pallas kernels for 0%

commit v1 on v0

--- a/solution.py
+++ b/solution.py
@@ -49,7 +49,19 @@
         part = lax.all_to_all(flipped, "dn", split_axis=1, concat_axis=0, tiled=True)
         whole = part.reshape(part.shape[0], part.shape[2])
         hopped = hop_lead(whole, signed, tile_columns).reshape(part.shape)
-        returned = lax.all_to_all(hopped, "dn", split_axis=0, concat_axis=1, tiled=True)
+        val = lax.axis_size("dn")
+        prior = lax.axis_index("dn")
+        u1, piece_now = (val, prior)
+        val2 = hopped.shape[0] // u1
+        raw_out = jnp.roll(hopped, -piece_now * val2, axis=0)
+        piece_out = lax.slice_in_dim(raw_out, 0, val2, axis=0)
+        grid = [piece_out]
+        for s in [*range(1, u1)]:
+            state_now = lax.slice_in_dim(raw_out, s * val2, (s + 1) * val2, axis=0)
+            r2 = lax.ppermute(state_now, "dn", [(q, (q + s) % u1) for q in range(u1)])
+            grid.append(r2)
+        tmp = jnp.concatenate(grid[::-1], axis=1)
+        returned = jnp.roll(tmp, shift=(piece_now + 1) * grid[0].shape[1], axis=1)
         hopped_down = returned.reshape(block_cols, block_rows).T
         work = (
             hopped_up.astype(jnp.float32)

time: 2630 us -> 2200 us (0.84)
  local copies, waits for them, and re-layouts: 1360 us -> 928 us
  waiting for transfers between devices: 194 us -> 329 us
  other arithmetic: 469 us -> 346 us
    ppermute x0 -> x6, waiting for transfers between devices: none -> 329 us  [body(): r2 = lax.ppermute(state_now, 'dn', [(q, (q + s) % u1) for q in range(u1)])]
    all_to_all x2 -> x0, waiting for transfers between devices: 194 us -> none  [body(): lax.all_to_all(hopped, 'dn', split_axis=0, concat_axis=1, tiled=True)]
    convert_element_type x4 -> x2, other arithmetic: 350 us -> 175 us  [hop_lead(): return result.reshape(layout).astype(jnp.bfloat16)]
    unnamed x22 -> x18, local copies, waits for them, and re-layouts: 257 us -> 122 us
    convert_element_type x9, local copies, waits for them, and re-layouts: 376 us -> 260 us  [hop_lead(): return result.reshape(layout).astype(jnp.bfloat16)]
    all_to_all x2 -> x0, local copies, waits for them, and re-layouts: 106 us -> none  [body(): lax.all_to_all(hopped, 'dn', split_axis=0, concat_axis=1, tiled=True)]
    convert_element_type x4 -> x0, local copies, waits for them, and re-layouts: 81.9 us -> none  [body(): hopped_down.astype(jnp.float32)]
    concatenate x0 -> x4, other arithmetic: none -> 54.9 us  [the longest x2 33.2 us: body(): returned = jnp.roll(tmp, shift=(piece_now + 1) * grid[0].shape[1], axis=1)]
  transfers between devices with their start and end apart: 6 -> 10, of which waited for: 2 -> 5; matrix products, arithmetic and copies ran while one was open for 59% -> 50% of each run, Pallas kernels for 0% -> 0%
where the time goes in v1:
time: 2200 us; the launch traced here: 2180 us
  local copies, waits for them, and re-layouts  928 us (42%)
  blocking collectives  378 us (17%)
  other arithmetic  346 us (16%)
  waiting for transfers between devices  329 us (15%)
  matrix products  148 us (7%)
  starting transfers between devices  39.4 us (2%)
    ppermute x6, waiting for transfers between devices, body(): r2 = lax.ppermute(state_now, 'dn', [(q, (q + s) % u1) for q in range(u1)])  329 us
    convert_element_type x9, local copies, waits for them, and re-layouts, hop_lead(): return result.reshape(layout).astype(jnp.bfloat16)  260 us
    all_to_all x2, blocking collectives, body(): lax.all_to_all(cube, 'up', split_axis=1, concat_axis=0, tiled=True)  254 us
    convert_element_type x2, other arithmetic, hop_lead(): return result.reshape(layout).astype(jnp.bfloat16)  175 us
    another operation x8, local copies, waits for them, and re-layouts, hop_lead(): cube = matrix.reshape(layout[0] // tile_width, tile_width, -1)  122 us
    unnamed x18, local copies, waits for them, and re-layouts  122 us
    dot_general x4, matrix products, hop_lead(): jnp.einsum('ikab,ikbm->iam', signed, picked, preferred_element_type=jnp.f...  118 us
    gather x4, local copies, waits for them, and re-layouts, hop_lead(): picked = cube[tile_columns]  106 us
  transfers between devices with their start and end apart: 10, of which 5 were waited for; matrix products, arithmetic and copies ran while one was open for 50% of the time, Pallas kernels for 0%

profile of v1, /device:TPU:12, one launch (start us, length us, event | category | flops | bytes accessed | tf_op | source)
XLA Modules:
  0.0 2177.8 jit_solution(12280559423834406255)
XLA Ops:
  11.1 41.6 %psum.35 = f32[]{:T(128)} all-reduce(f32[]{:T(128)} %fusion), channel_id=1, replica_groups=mesh['up'=8,'dn'=4] {'up','dn'}, use_global_device_ids=true, to_apply=%region_1.0 | all-reduce | flops 1 | bytes 8 | tf_op jit(solution)/shard_map/psum | solution.py:33
  80.3 127.1 %all_to_all.78 = bf16[1664,8,416]{0,2,1:T(8,128)(2,1)} all-to-all(bf16[1664,8,416]{0,2,1:T(8,128)(2,1)} %bitcast.116), channel_id=1, replica_groups=mesh['up'=8,'dn'=4] {'up'}, dimensions={1} | all-to-all | bytes 22151168 | tf_op jit(solution)/shard_map/all_to_all | solution.py:43
  291.6 29.5 %bitcast_convert_fusion.3 = bf16[104,128,416]{1,2,0:T(8,128)(2,1)} fusion(bf16[104,5,128,416]{2,3,1,0:T(8,128)(2,1)} %bitcast.111, bf16[104,5,128,128]{3,2,1,0:T(8,128)(2,1)} %param.10, bf16[104,5]{1,0:T(8,128)(2,1)S(1)} %copy.53), kind=kOutput, calls=%fused_computation.37 | convolution fusion | flops 7102431232 | bytes 83493904 | tf_op jit(solution)/shard_map/ikab,ikbm->iam/dot_general | solution.py:15
  337.4 77.8 %reshape.147 = bf16[13312,1,416]{2,1,0:T(2,128)(2,1)} reshape(bf16[104,128,416]{2,1,0:T(8,128)(2,1)} %copy.81) | data formatting | bytes 22151168 | tf_op jit(solution)/shard_map/convert_element_type | solution.py:16
  415.7 87.5 %reduce = bf16[13312,416]{1,0:T(8,128)(2,1)} reduce(bf16[13312,1,416]{2,1,0:T(2,128)(2,1)} %reshape.147, bf16[]{:T(256)} %broadcast.22), dimensions={1}, to_apply=%reshape.147.reduce_sub_computation | reduce | bytes 22151170 | tf_op jit(solution)/shard_map/convert_element_type | solution.py:16
  614.0 29.4 %bitcast_convert_fusion.2 = bf16[104,128,416]{1,2,0:T(8,128)(2,1)} fusion(bf16[104,5,128,416]{2,3,1,0:T(8,128)(2,1)} %bitcast.112, bf16[104,5,128,128]{3,2,1,0:T(8,128)(2,1)} %param.10, bf16[104,5]{1,0:T(8,128)(2,1)S(1)} %copy.53), kind=kOutput, calls=%fused_computation.36 | convolution fusion | flops 7102431232 | bytes 83493904 | tf_op jit(solution)/shard_map/ikab,ikbm->iam/dot_general | solution.py:15
  699.7 30.6 %reshape.150 = bf16[13312,1,416]{2,1,0:T(2,128)(2,1)} reshape(bf16[8,2,346112]{2,1,0:T(2,128)(2,1)} %all-to-all-done.1) | data formatting | bytes 22151168
  730.3 52.5 %copy.60 = bf16[13312,1,416]{0,2,1:T(8,128)(2,1)} copy(bf16[13312,1,416]{2,1,0:T(2,128)(2,1)} %reshape.150) | data formatting | bytes 22151168 | tf_op jit(solution)/shard_map/all_to_all | solution.py:46
  840.2 34.8 %collective-permute-done.1 = bf16[3328,1,416]{0,2,1:T(8,128)(2,1)} collective-permute-done((bf16[3328,1,416]{0,2,1:T(8,128)(2,1)}, bf16[3328,1,416]{0,2,1:T(8,128)(2,1)}, u32[]{:S(2)}, u32[]{:S(2)}) %collective-permute-start.1) | collective-permute-done | bytes 2768928 | tf_op jit(solution)/shard_map/ppermute | solution.py:61
  875.0 58.7 %collective-permute-done.2 = bf16[3328,1,416]{0,2,1:T(8,128)(2,1)} collective-permute-done((bf16[3328,1,416]{0,2,1:T(8,128)(2,1)}, bf16[3328,1,416]{0,2,1:T(8,128)(2,1)}, u32[]{:S(2)}, u32[]{:S(2)}) %collective-permute-start.2) | collective-permute-done | bytes 2768928 | tf_op jit(solution)/shard_map/ppermute | solution.py:61
  950.2 29.9 %multiply_reduce_fusion.3 = (f32[]{:T(128)}, f32[]{:T(128)}, f32[1664,3328]{1,0:T(8,128)}, f32[1664,3328]{1,0:T(8,128)}) fusion(f32[]{:T(128)S(6)} %max.13, bf16[1664,3328]{1,0:T(8,128)(2,1)} %param.9, f32[1664,3328]{1,0:T(8,128)} %copy.65, bf16[3328,4,416]{0,2,1:T(8,128)(2,1)} %fusion.17, s32[16,13312]{1,0:T(8,128)} %param.13, s32[]{:T(128)S(6)} %select_n.31, ...), kind=kOutput, calls=%fused_computation.43 | convolution fusion | flops 238204928 | bytes 88924176 | tf_op jit(solution)/shard_map/sa,sb->ab/dot_general | solution.py:29
  980.0 41.1 %all-reduce.1 = (f32[]{:T(128)}, f32[]{:T(128)}) all-reduce(f32[]{:T(128)} %get-tuple-element.8, f32[]{:T(128)} %get-tuple-element.7), channel_id=1, replica_groups=mesh['up'=8,'dn'=4] {'up','dn'}, use_global_device_ids=true, to_apply=%region_5.8 | all-reduce | flops 2 | bytes 16 | tf_op jit(solution)/shard_map/psum | solution.py:72
  1063.4 127.0 %all_to_all.79 = bf16[1664,8,416]{0,2,1:T(8,128)(2,1)} all-to-all(bf16[1664,8,416]{0,2,1:T(8,128)(2,1)} %bitcast.117), channel_id=1, replica_groups=mesh['up'=8,'dn'=4] {'up'}, dimensions={1} | all-to-all | bytes 22151168 | tf_op jit(solution)/shard_map/all_to_all | solution.py:43
  1275.7 29.4 %bitcast_convert_fusion.1 = bf16[104,128,416]{1,2,0:T(8,128)(2,1)} fusion(bf16[104,5,128,416]{2,3,1,0:T(8,128)(2,1)} %bitcast.113, bf16[104,5,128,128]{3,2,1,0:T(8,128)(2,1)} %param.10, bf16[104,5]{1,0:T(8,128)(2,1)S(1)} %copy-done.3), kind=kOutput, calls=%fused_computation.35 | convolution fusion | flops 7102431232 | bytes 83493904 | tf_op jit(solution)/shard_map/ikab,ikbm->iam/dot_general | solution.py:15
  1321.4 77.7 %reshape.148 = bf16[13312,1,416]{2,1,0:T(2,128)(2,1)} reshape(bf16[104,128,416]{2,1,0:T(8,128)(2,1)} %copy.82) | data formatting | bytes 22151168 | tf_op jit(solution)/shard_map/convert_element_type | solution.py:16
  1399.1 87.5 %reduce.1 = bf16[13312,416]{1,0:T(8,128)(2,1)} reduce(bf16[13312,1,416]{2,1,0:T(2,128)(2,1)} %reshape.148, bf16[]{:T(256)} %broadcast.22), dimensions={1}, to_apply=%reshape.148.reduce_sub_computation | reduce | bytes 22151170 | tf_op jit(solution)/shard_map/convert_element_type | solution.py:16
  1597.0 29.4 %bitcast_convert_fusion = bf16[104,128,416]{1,2,0:T(8,128)(2,1)} fusion(bf16[104,5,128,416]{2,3,1,0:T(8,128)(2,1)} %bitcast.110, bf16[104,5,128,128]{3,2,1,0:T(8,128)(2,1)} %param.10, bf16[104,5]{1,0:T(8,128)(2,1)S(1)} %copy-done.3), kind=kOutput, calls=%fused_computation.34 | convolution fusion | flops 7102431232 | bytes 83493904 | tf_op jit(solution)/shard_map/ikab,ikbm->iam/dot_general | solution.py:15
  1681.6 58.7 %collective-permute-done.3 = bf16[3328,1,416]{0,2,1:T(8,128)(2,1)} collective-permute-done((bf16[3328,1,416]{0,2,1:T(8,128)(2,1)}, bf16[3328,1,416]{0,2,1:T(8,128)(2,1)}, u32[]{:S(2)}, u32[]{:S(2)}) %collective-permute-start.3) | collective-permute-done | bytes 2768928 | tf_op jit(solution)/shard_map/ppermute | solution.py:61
  1740.3 117.9 %collective-permute-done.4 = bf16[3328,1,416]{0,2,1:T(8,128)(2,1)} collective-permute-done((bf16[3328,1,416]{0,2,1:T(8,128)(2,1)}, bf16[3328,1,416]{0,2,1:T(8,128)(2,1)}, u32[]{:S(2)}, u32[]{:S(2)}) %collective-permute-start.4) | collective-permute-done | bytes 2768928 | tf_op jit(solution)/shard_map/ppermute | solution.py:61
  1858.2 58.7 %collective-permute-done.5 = bf16[3328,1,416]{0,2,1:T(8,128)(2,1)} collective-permute-done((bf16[3328,1,416]{0,2,1:T(8,128)(2,1)}, bf16[3328,1,416]{0,2,1:T(8,128)(2,1)}, u32[]{:S(2)}, u32[]{:S(2)}) %collective-permute-start.5) | collective-permute-done | bytes 2768928 | tf_op jit(solution)/shard_map/ppermute | solution.py:61
  1933.7 30.4 %reshape.152 = bf16[13312,1,416]{2,1,0:T(2,128)(2,1)} reshape(bf16[8,2,346112]{2,1,0:T(2,128)(2,1)} %all-to-all-done.4) | data formatting | bytes 22151168
  1964.1 52.5 %copy.71 = bf16[13312,1,416]{0,2,1:T(8,128)(2,1)} copy(bf16[13312,1,416]{2,1,0:T(2,128)(2,1)} %reshape.152) | data formatting | bytes 22151168 | tf_op jit(solution)/shard_map/all_to_all | solution.py:46
  2074.0 37.2 %multiply_reduce_fusion.1 = (f32[]{:T(128)}, f32[]{:T(128)}, f32[1664,3328]{1,0:T(8,128)}) fusion(f32[1664,3328]{1,0:T(8,128)} %get-tuple-element.15, f32[]{:T(128)S(6)} %max.13, bf16[1664,3328]{1,0:T(8,128)(2,1)} %param.9, f32[]{:T(128)} %sqrt.10, f32[1664,3328]{1,0:T(8,128)} %get-tuple-element.25, f32[1664,3328]{1,0:T(8,128)} %copy.76, ...), kind=kLoop, calls=%fused_computation.40 | loop fusion | flops 71991296 | bytes 110755856 | tf_op jit(solution)/shard_map/reduce_sum | solution.py:72
  2111.2 41.2 %all-reduce = (f32[]{:T(128)}, f32[]{:T(128)}) all-reduce(f32[]{:T(128)} %get-tuple-element.6, f32[]{:T(128)} %get-tuple-element.5), channel_id=1, replica_groups=mesh['up'=8,'dn'=4] {'up','dn'}, use_global_device_ids=true, to_apply=%region_9.12 | all-reduce | flops 2 | bytes 16 | tf_op jit(solution)/shard_map/psum | solution.py:72
  (79 shorter events, 779.8 us)
Async XLA Ops:
  80.3 133.9 %copy-start.5 = (s32[104,5]{0,1:T(8,128)S(1)}, s32[104,5]{0,1:T(8,128)}, u32[]{:S(2)}) copy-start(s32[104,5]{0,1:T(8,128)} %param.11) | copy-start | bytes 6244
  80.3 134.2 %copy-start.4 = (s32[104,5]{0,1:T(8,128)S(1)}, s32[104,5]{0,1:T(8,128)}, u32[]{:S(2)}) copy-start(s32[104,5]{0,1:T(8,128)} %param.12) | copy-start | bytes 6244
  207.5 317.5 %all-to-all-start.2 = ((bf16[3328,4,416]{0,2,1:T(8,128)(2,1)}), bf16[3328,4,416]{0,2,1:T(8,128)(2,1)}, u32[]{:S(2)}, u32[]{:S(2)}) async-start(bf16[3328,4,416]{0,2,1:T(8,128)(2,1)} %bitcast.102), calls=%async_computation.2 | async-start | bytes 22151168 | tf_op jit(solution)/shard_map/all_to_all | solution.py:49
  214.7 399.3 %copy-start.2 = (bf16[104,5]{1,0:T(8,128)(2,1)}, bf16[104,5]{1,0:T(8,128)(2,1)S(1)}, u32[]{:S(2)}) copy-start(bf16[104,5]{1,0:T(8,128)(2,1)S(1)} %copy.53) | copy-start | bytes 3124
  214.7 372.8 %copy-start = (s32[1024]{0:T(1024)}, s32[1024]{0:T(1024)S(1)}, u32[]{:S(2)}) copy-start(s32[1024]{0:T(1024)S(1)} %pad_clamp_fusion) | copy-start | bytes 12292
  524.9 174.7 %all-to-all-start.1 = ((bf16[8,2,346112]{2,1,0:T(2,128)(2,1)}), bf16[8,2,346112]{2,1,0:T(2,128)(2,1)}, u32[]{:S(2)}, u32[]{:S(2)}) async-start(bf16[8,2,346112]{2,1,0:T(2,128)(2,1)} %reshape.149), calls=%async_computation.1 | async-start | bytes 22151168 | tf_op jit(solution)/shard_map/all_to_all | solution.py:46
  693.1 147.1 %collective-permute-start = (bf16[3328,1,416]{0,2,1:T(8,128)(2,1)}, bf16[3328,1,416]{0,2,1:T(8,128)(2,1)}, u32[]{:S(2)}, u32[]{:S(2)}) collective-permute-start(bf16[3328,1,416]{0,2,1:T(8,128)(2,1)} %get-tuple-element.24), channel_id=1, source_target_pairs={{0,3},{1,0},{2,1},{3,2},{4,7},{5,4},{6,5},{7,6},{8,11},{9,8},{10,9... | collective-permute-start | bytes 8306696 | tf_op jit(solution)/shard_map/ppermute | solution.py:61
  693.2 181.9 %collective-permute-start.1 = (bf16[3328,1,416]{0,2,1:T(8,128)(2,1)}, bf16[3328,1,416]{0,2,1:T(8,128)(2,1)}, u32[]{:S(2)}, u32[]{:S(2)}) collective-permute-start(bf16[3328,1,416]{0,2,1:T(8,128)(2,1)} %get-tuple-element.23), channel_id=1, source_target_pairs={{0,2},{1,3},{2,0},{3,1},{4,6},{5,7},{6,4},{7,5},{8,10},{9,11},{10,... | collective-permute-start | bytes 8306696 | tf_op jit(solution)/shard_map/ppermute | solution.py:61
  696.1 237.7 %collective-permute-start.2 = (bf16[3328,1,416]{0,2,1:T(8,128)(2,1)}, bf16[3328,1,416]{0,2,1:T(8,128)(2,1)}, u32[]{:S(2)}, u32[]{:S(2)}) collective-permute-start(bf16[3328,1,416]{0,2,1:T(8,128)(2,1)} %get-tuple-element.22), channel_id=1, source_target_pairs={{0,1},{1,2},{2,3},{3,0},{4,5},{5,6},{6,7},{7,4},{8,9},{9,10},{10,1... | collective-permute-start | bytes 8306696 | tf_op jit(solution)/shard_map/ppermute | solution.py:61
  1190.4 317.9 %all-to-all-start.5 = ((bf16[3328,4,416]{0,2,1:T(8,128)(2,1)}), bf16[3328,4,416]{0,2,1:T(8,128)(2,1)}, u32[]{:S(2)}, u32[]{:S(2)}) async-start(bf16[3328,4,416]{0,2,1:T(8,128)(2,1)} %bitcast.103), calls=%async_computation.5 | async-start | bytes 22151168 | tf_op jit(solution)/shard_map/all_to_all | solution.py:49
  1217.4 31.8 %copy-start.1 = (s32[1024]{0:T(1024)S(1)}, s32[1024]{0:T(1024)}, u32[]{:S(2)}) copy-start(s32[1024]{0:T(1024)} %copy-done) | copy-start | bytes 12292
  1249.2 26.5 %copy-start.3 = (bf16[104,5]{1,0:T(8,128)(2,1)S(1)}, bf16[104,5]{1,0:T(8,128)(2,1)}, u32[]{:S(2)}) copy-start(bf16[104,5]{1,0:T(8,128)(2,1)} %copy-done.2) | copy-start | bytes 3124
  1508.3 425.4 %all-to-all-start.4 = ((bf16[8,2,346112]{2,1,0:T(2,128)(2,1)}), bf16[8,2,346112]{2,1,0:T(2,128)(2,1)}, u32[]{:S(2)}, u32[]{:S(2)}) async-start(bf16[8,2,346112]{2,1,0:T(2,128)(2,1)} %reshape.151), calls=%async_computation.4 | async-start | bytes 22151168 | tf_op jit(solution)/shard_map/all_to_all | solution.py:46
  1676.3 64.0 %collective-permute-start.3 = (bf16[3328,1,416]{0,2,1:T(8,128)(2,1)}, bf16[3328,1,416]{0,2,1:T(8,128)(2,1)}, u32[]{:S(2)}, u32[]{:S(2)}) collective-permute-start(bf16[3328,1,416]{0,2,1:T(8,128)(2,1)} %get-tuple-element.20), channel_id=1, source_target_pairs={{0,3},{1,0},{2,1},{3,2},{4,7},{5,4},{6,5},{7,6},{8,11},{9,8},{10,9... | collective-permute-start | bytes 8306696 | tf_op jit(solution)/shard_map/ppermute | solution.py:61
  1676.3 181.9 %collective-permute-start.4 = (bf16[3328,1,416]{0,2,1:T(8,128)(2,1)}, bf16[3328,1,416]{0,2,1:T(8,128)(2,1)}, u32[]{:S(2)}, u32[]{:S(2)}) collective-permute-start(bf16[3328,1,416]{0,2,1:T(8,128)(2,1)} %get-tuple-element.19), channel_id=1, source_target_pairs={{0,2},{1,3},{2,0},{3,1},{4,6},{5,7},{6,4},{7,5},{8,10},{9,11},{10,... | collective-permute-start | bytes 8306696 | tf_op jit(solution)/shard_map/ppermute | solution.py:61
  1679.2 237.7 %collective-permute-start.5 = (bf16[3328,1,416]{0,2,1:T(8,128)(2,1)}, bf16[3328,1,416]{0,2,1:T(8,128)(2,1)}, u32[]{:S(2)}, u32[]{:S(2)}) collective-permute-start(bf16[3328,1,416]{0,2,1:T(8,128)(2,1)} %get-tuple-element.18), channel_id=1, source_target_pairs={{0,1},{1,2},{2,3},{3,0},{4,5},{5,6},{6,7},{7,4},{8,9},{9,10},{10,1... | collective-permute-start | bytes 8306696 | tf_op jit(solution)/shard_map/ppermute | solution.py:61
